TPU v7x, 256 devices: a whole 4x4x8 slice. The times are simulated.
256 devices in a mesh: lon: 64 (over x, z_hi, y, core), lat: 4 (over z_lo).
Axes of the slice: x: 4, y: 4, z: 8 (z_hi: 2, z_lo: 4; z = z_hi * 4 + z_lo), core: 2. Of those that a mesh axis runs over, the one named last changes fastest.
Arguments:
- fields: bfloat16 [4, 128, 256, 8192], P(None, None, 'lat', 'lon'), may hold values from -12 to 12
- bracket: int32 [32, 256, 8192], P(None, 'lat', 'lon'), may hold values from 0 to 126, as said below
- fraction: bfloat16 [32, 256, 8192], P(None, 'lat', 'lon'), may hold values from 0 to 1
Outputs:
- on_pressure: bfloat16 [4, 32, 256, 8192], P(None, None, ('lat', 'lon'))
- zonal_mean: float32 [4, 32, 256], P(None, None, ('lat', 'lon'))
- meridional: float32 [4, 32, 256], P(None, None, ('lat', 'lon'))
Inputs may be any that keep to these rules, and one draw needn't show every extreme that they name: bracket[p, r, c] - min(p * 4, 112) lies in 0 to 14 for every column, and each of these offsets occurs.
All inputs are finite; a program needn't handle non-finite values.
Results may differ from a plain program's by a relative error of at most 0.0012.
Values may be sent and summed in bfloat16 or wider, within the bound.
A program may use at most 128 MiB of HBM per device.

v0:
```python
import jax
import jax.numpy as jnp
from jax import lax
from jax.sharding import Mesh
from jax.sharding import PartitionSpec as P

WINDOW = 16
LON = ("lon_0", "lon_1", "lon_2", "lon_3")
LAT_LON = ("lat", "lon_0", "lon_1", "lon_2", "lon_3")


def split_up(x, dim, peers):
    shape = x.shape
    blocks = x.reshape(*shape[:dim], peers, shape[dim] // peers, *shape[dim + 1 :])
    return jnp.moveaxis(blocks, dim, 0)


def joined_along(blocks, dim):
    blocks = jnp.moveaxis(blocks, 0, dim)
    shape = blocks.shape
    return blocks.reshape(*shape[:dim], shape[dim] * shape[dim + 1], *shape[dim + 2 :])


def exchange_in_order(blocks, axes, turns):
    inside = blocks.shape[1:]
    result = blocks.reshape(*(lax.axis_size(a) for a in axes), *inside)
    for k in turns:
        result = lax.all_to_all(result, axes[k], k, k, tiled=True)
    return result.reshape(-1, *inside)


def two_step_exchange(x, groups, turns, split_dim, concat_dim):
    peers = lax.axis_size(groups[0]) * lax.axis_size(groups[1])
    blocks = split_up(x, split_dim, peers)
    return joined_along(exchange_in_order(blocks, groups, turns), concat_dim)


def shifted(value, axis, steps):
    count = lax.axis_size(axis)
    pairs = [(source, (source + steps) % count) for source in range(count)]
    return lax.ppermute(value, axis, pairs)


def shifted_2(block, axis, distance):
    devices = range(lax.axis_size(axis))
    route = [(i - distance, i) for i in devices if i - distance in devices]
    return lax.ppermute(block, axis, route)


def interpolate(block, bracket, fraction):
    level_count = block.shape[1]
    plev_count = bracket.shape[0]
    level_step = level_count // plev_count
    group_size = min(8, plev_count)
    group_count = plev_count // group_size
    steps = jnp.arange(WINDOW, dtype=jnp.int32).reshape(1, WINDOW, 1, 1)

    def one_level(pressure, level_index, weight):
        window_base = jnp.minimum(pressure * level_step, level_count - WINDOW)
        window = lax.dynamic_slice_in_dim(block, window_base, WINDOW, 1)
        offset = (level_index - window_base)[None, None]
        zero = jnp.zeros((), jnp.bfloat16)
        lower_level = jnp.sum(jnp.where(steps == offset, window, zero).astype(jnp.float32), axis=1)
        upper_level = jnp.sum(
            jnp.where(steps == offset + 1, window, zero).astype(jnp.float32), axis=1
        )
        scale = weight.astype(jnp.float32)[None]
        return (lower_level + scale * (upper_level - lower_level)).astype(jnp.bfloat16)

    def one_group(packed):
        pressures, level_group, weight_group = packed
        return jax.vmap(one_level, in_axes=(0, 0, 0), out_axes=1)(
            pressures, level_group, weight_group
        )

    pressure_ids = jnp.arange(plev_count, dtype=jnp.int32).reshape(group_count, group_size)
    level_groups = bracket.reshape((group_count, group_size) + bracket.shape[1:])
    weight_groups = fraction.reshape((group_count, group_size) + fraction.shape[1:])
    grouped = lax.map(one_group, (pressure_ids, level_groups, weight_groups))
    grouped = jnp.moveaxis(grouped, 0, 1)
    return grouped.reshape((block.shape[0], plev_count) + bracket.shape[1:])


def shards(fields, bracket, fraction):
    local_levels = interpolate(fields, bracket, fraction)
    on_pressure = two_step_exchange(
        local_levels, (("lon_0", "lon_1", "lon_2"), "lon_3"), (0, 1), 2, 3
    )
    total_lon = on_pressure.shape[3]
    zonal_mean = jnp.sum(on_pressure.astype(jnp.float32), axis=3) / jnp.float32(total_lon)
    lon_count = lax.axis_size(LON)
    lon_place = lax.axis_index(LON)
    from_prev = shifted(zonal_mean, LON, 1)
    from_next = shifted(zonal_mean, LON, -1)
    cross_prev = shifted_2(from_prev, "lat", 1)
    cross_next = shifted_2(from_next, "lat", -1)
    below_row = jnp.where(lon_place == 0, cross_prev, from_prev)
    above_row = jnp.where(lon_place == lon_count - 1, cross_next, from_next)
    padded = jnp.concatenate([below_row, zonal_mean, above_row], axis=2)
    own_rows = zonal_mean.shape[2]
    owner_place = lax.axis_index("lat") * lon_count + lon_place
    row_index = owner_place * own_rows + jnp.arange(own_rows, dtype=jnp.int32)
    last_index = lax.axis_size("lat") * lon_count * own_rows - 1
    centered = 0.5 * (padded[:, :, 2:] - padded[:, :, :-2])
    forward = padded[:, :, 2:] - padded[:, :, 1:-1]
    backward = padded[:, :, 1:-1] - padded[:, :, :-2]
    meridional = jnp.where(
        row_index == 0, forward, jnp.where(row_index == last_index, backward, centered)
    )
    return (on_pressure, zonal_mean, meridional)


def solution(mesh):
    finer = Mesh(
        mesh.devices.reshape(4, 2, 4, 2, mesh.shape["lat"]),
        ("lon_0", "lon_1", "lon_2", "lon_3", "lat"),
    )
    in_specs = (P(None, None, "lat", LON), P(None, "lat", LON), P(None, "lat", LON))
    out_specs = (P(None, None, LAT_LON, None), P(None, None, LAT_LON), P(None, None, LAT_LON))
    return jax.shard_map(
        shards, mesh=finer, in_specs=in_specs, out_specs=out_specs, check_vma=False
    )
```

profile of v0, /device:TPU:32, one launch (start us, length us, event | category | flops | bytes accessed | tf_op | source)
XLA Modules:
  0.0 184.4 jit_solution(7617257096810461066)
XLA Ops:
  0.7 9.6 %copy.26 = bf16[4,128,64,128]{3,2,0,1:T(8,128)(2,1)} copy(bf16[4,128,64,128]{3,2,1,0:T(8,128)(2,1)} %param.5) | data formatting | bytes 16777216
  10.3 74.9 %while.12 = (s32[]{:T(128)}, bf16[4,4,8,64,128]{4,3,2,0,1:T(8,128)(2,1)S(1)}, s32[4,8,64,128]{3,2,1,0:T(8,128)}, s32[4,8]{1,0:T(4,128)S(1)}, bf16[4,128,64,128]{...) while((s32[]{:T(128)}, bf16[4,4,8,64,128]{4,3,2,0,1:T(8,128)(2,1)S(1)}, ...), condition=%wide.region_3.4_spmd.clone.clone, body=%wide.region_0.3_spmd.clone.clone.sunk | while | flops 27983944 | bytes 36045192 | solution.py:79
  10.3 8.2 %gather_fusion = bf16[8,4,16,64,128]{4,3,1,2,0:T(8,128)(2,1)} fusion(bf16[4,128,64,128]{3,2,0,1:T(8,128)(2,1)} %get-tuple-element.208, s32[8]{0:T(128)S(1)} %fusion.18), kind=kCustom, calls=%fused_computation.clone.clone.1 | custom fusion | bytes 16777344 | tf_op jit(solution)/shard_map/while/body/eval_jaxpr/vmap()/gather | solution.py:60
  18.5 1.1 broadcast_add_fusion.2
  19.5 1.2 iota_compare_fusion.3
  20.7 7.1 %convert_reduce_fusion.4 = (f32[8,4,64,128]{3,2,1,0:T(8,128)S(1)}, f32[8,4,64,128]{3,2,1,0:T(8,128)S(1)}) fusion(bf16[8,4,16,64,128]{4,3,1,2,0:T(8,128)(2,1)} %gather_fusion, pred[8,16,64,128]{3,2,1,0:T(8,128)(4,1)S(1)} %get-tuple-element.186, pred[8,16,64,128]{3,2,1,0:T(8,128)(4,1)S(1)} %get-tuple-element.187), kind=kLoop, calls=%fused_computation.3.clone.1 | loop fusion | flops 24641536 | bytes 12582912 | tf_op jit(solution)/shard_map/while/body/eval_jaxpr/vmap()/reduce_sum | solution.py:63
  27.8 0.9 bitcast_convert_fusion.2
  28.7 0.3 copy_dynamic-update-slice_fusion.2
  29.0 8.2 %gather_fusion = bf16[8,4,16,64,128]{4,3,1,2,0:T(8,128)(2,1)} fusion(bf16[4,128,64,128]{3,2,0,1:T(8,128)(2,1)} %get-tuple-element.208, s32[8]{0:T(128)S(1)} %fusion.18), kind=kCustom, calls=%fused_computation.clone.clone.1 | custom fusion | bytes 16777344 | tf_op jit(solution)/shard_map/while/body/eval_jaxpr/vmap()/gather | solution.py:60
  37.2 1.1 broadcast_add_fusion.2
  38.2 1.2 iota_compare_fusion.3
  39.4 7.1 %convert_reduce_fusion.4 = (f32[8,4,64,128]{3,2,1,0:T(8,128)S(1)}, f32[8,4,64,128]{3,2,1,0:T(8,128)S(1)}) fusion(bf16[8,4,16,64,128]{4,3,1,2,0:T(8,128)(2,1)} %gather_fusion, pred[8,16,64,128]{3,2,1,0:T(8,128)(4,1)S(1)} %get-tuple-element.186, pred[8,16,64,128]{3,2,1,0:T(8,128)(4,1)S(1)} %get-tuple-element.187), kind=kLoop, calls=%fused_computation.3.clone.1 | loop fusion | flops 24641536 | bytes 12582912 | tf_op jit(solution)/shard_map/while/body/eval_jaxpr/vmap()/reduce_sum | solution.py:63
  46.5 0.9 bitcast_convert_fusion.2
  47.4 0.3 copy_dynamic-update-slice_fusion.2
  47.7 8.2 %gather_fusion = bf16[8,4,16,64,128]{4,3,1,2,0:T(8,128)(2,1)} fusion(bf16[4,128,64,128]{3,2,0,1:T(8,128)(2,1)} %get-tuple-element.208, s32[8]{0:T(128)S(1)} %fusion.18), kind=kCustom, calls=%fused_computation.clone.clone.1 | custom fusion | bytes 16777344 | tf_op jit(solution)/shard_map/while/body/eval_jaxpr/vmap()/gather | solution.py:60
  55.9 1.1 broadcast_add_fusion.2
  57.0 1.2 iota_compare_fusion.3
  58.1 7.1 %convert_reduce_fusion.4 = (f32[8,4,64,128]{3,2,1,0:T(8,128)S(1)}, f32[8,4,64,128]{3,2,1,0:T(8,128)S(1)}) fusion(bf16[8,4,16,64,128]{4,3,1,2,0:T(8,128)(2,1)} %gather_fusion, pred[8,16,64,128]{3,2,1,0:T(8,128)(4,1)S(1)} %get-tuple-element.186, pred[8,16,64,128]{3,2,1,0:T(8,128)(4,1)S(1)} %get-tuple-element.187), kind=kLoop, calls=%fused_computation.3.clone.1 | loop fusion | flops 24641536 | bytes 12582912 | tf_op jit(solution)/shard_map/while/body/eval_jaxpr/vmap()/reduce_sum | solution.py:63
  65.2 0.9 bitcast_convert_fusion.2
  66.2 0.3 copy_dynamic-update-slice_fusion.2
  66.5 8.2 %gather_fusion = bf16[8,4,16,64,128]{4,3,1,2,0:T(8,128)(2,1)} fusion(bf16[4,128,64,128]{3,2,0,1:T(8,128)(2,1)} %get-tuple-element.208, s32[8]{0:T(128)S(1)} %fusion.18), kind=kCustom, calls=%fused_computation.clone.clone.1 | custom fusion | bytes 16777344 | tf_op jit(solution)/shard_map/while/body/eval_jaxpr/vmap()/gather | solution.py:60
  74.6 1.1 broadcast_add_fusion.2
  75.7 1.2 iota_compare_fusion.3
  76.9 7.1 %convert_reduce_fusion.4 = (f32[8,4,64,128]{3,2,1,0:T(8,128)S(1)}, f32[8,4,64,128]{3,2,1,0:T(8,128)S(1)}) fusion(bf16[8,4,16,64,128]{4,3,1,2,0:T(8,128)(2,1)} %gather_fusion, pred[8,16,64,128]{3,2,1,0:T(8,128)(4,1)S(1)} %get-tuple-element.186, pred[8,16,64,128]{3,2,1,0:T(8,128)(4,1)S(1)} %get-tuple-element.187), kind=kLoop, calls=%fused_computation.3.clone.1 | loop fusion | flops 24641536 | bytes 12582912 | tf_op jit(solution)/shard_map/while/body/eval_jaxpr/vmap()/reduce_sum | solution.py:63
  84.0 0.9 bitcast_convert_fusion.2
  84.9 0.3 copy_dynamic-update-slice_fusion.2
  85.2 3.7 %copy.28 = bf16[32,2,4,32,1,128]{5,1,3,2,4,0:T(2,128)(2,1)} copy(bf16[32,2,4,32,1,128]{5,1,0,3,2,4:T(2,128)(2,1)S(1)} %bitcast.73) | data formatting | bytes 4194304 | tf_op jit(solution)/shard_map/reshape | solution.py:26
  88.9 13.0 %all-to-all-start = ((bf16[32,2,4,32,1,128]{5,1,3,2,4,0:T(2,128)(2,1)}), bf16[32,2,4,32,1,128]{5,1,3,2,4,0:T(2,128)(2,1)S(1)}, u32[]{:S(2)}, u32[]{:S(2)}) async-start(bf16[32,2,4,32,1,128]{5,1,3,2,4,0:T(2,128)(2,1)} %copy.28), calls=%async_computation | async-start | bytes 4194304 | tf_op jit(solution)/shard_map/all_to_all | solution.py:28
  101.9 53.8 %all-to-all-done = bf16[32,2,4,32,1,128]{5,1,3,2,4,0:T(2,128)(2,1)S(1)} async-done(((bf16[32,2,4,32,1,128]{5,1,3,2,4,0:T(2,128)(2,1)}), bf16[32,2,4,32,1,128]{5,1,3,2,4,0:T(2,128)(2,1)S(1)}, u32[]{:S(2)}, u32[]{:S(2)}) %all-to-all-start) | async-done | bytes 2097184 | tf_op jit(solution)/shard_map/all_to_all | solution.py:28
  155.7 1.4 copy.29
  157.1 5.4 %all_to_all.10 = bf16[32,2,4,32,1,128]{5,0,3,2,4,1:T(8,128)(2,1)S(1)} all-to-all(bf16[32,2,4,32,1,128]{5,0,3,2,4,1:T(8,128)(2,1)S(1)} %copy.29), channel_id=1, replica_groups=mesh['lon_0'=4,'lon_1'=2,'lon_2'=4,'lon_3'=2,'lat'=4] {'lon_3'}, dimensions={1} | all-to-all | bytes 4194304 | tf_op jit(solution)/shard_map/all_to_all | solution.py:28
  162.5 0.8 copy.30
  163.3 0.4 convert_reduce_fusion.2
  163.7 0.6 fusion.12
  164.3 0.1 collective-permute-start.2
  164.5 9.7 %collective-permute-start = (f32[4,32,1]{1,0,2:T(4,128)S(1)}, f32[4,32,1]{1,0,2:T(4,128)S(1)}, u32[]{:S(2)}, u32[]{:S(2)}) collective-permute-start(f32[4,32,1]{1,0,2:T(4,128)S(1)} %get-tuple-element.139), channel_id=1, source_target_pairs={{0,252},{4,0},{8,4},{12,8},{16,12},{20,16},{24,20},{28,24},{32,28}... | collective-permute-start | bytes 1544 | tf_op jit(solution)/shard_map/ppermute | solution.py:41
  174.2 1.3 collective-permute-done.2
  175.5 2.9 %collective-permute-start.3 = (f32[4,32,1]{1,0,2:T(4,128)S(1)}, f32[4,32,1]{1,0,2:T(4,128)S(1)}, u32[]{:S(2)}, u32[]{:S(2)}) collective-permute-start(f32[4,32,1]{1,0,2:T(4,128)S(1)} %collective-permute-done.2), channel_id=1, source_target_pairs={{0,1},{1,2},{2,3},{4,5},{5,6},{6,7},{8,9},{9,10},{10,11},{12,13},{... | collective-permute-start | bytes 1544 | tf_op jit(solution)/shard_map/ppermute | solution.py:47
  178.4 0.0 collective-permute-done
  178.4 2.9 %collective-permute-start.1 = (f32[4,32,1]{1,0,2:T(4,128)S(1)}, f32[4,32,1]{1,0,2:T(4,128)S(1)}, u32[]{:S(2)}, u32[]{:S(2)}) collective-permute-start(f32[4,32,1]{1,0,2:T(4,128)S(1)} %collective-permute-done), channel_id=1, source_target_pairs={{1,0},{2,1},{3,2},{5,4},{6,5},{7,6},{9,8},{10,9},{11,10},{13,12},{... | collective-permute-start | bytes 1544 | tf_op jit(solution)/shard_map/ppermute | solution.py:47
  181.3 1.9 %copy.40 = bf16[1,64,4,4,8,128]{5,4,1,3,2,0:T(8,128)(2,1)} copy(bf16[1,64,4,4,8,128]{5,4,3,2,1,0:T(8,128)(2,1)S(1)} %bitcast.71) | data formatting | bytes 4194304 | tf_op jit(solution)/shard_map/reshape | solution.py:21
  183.2 0.0 collective-permute-done.3
  183.2 0.7 collective-permute-done.1
  183.9 0.6 select_select_fusion
  (10 shorter events, 0.1 us)
Async XLA Ops:
  88.9 66.9 %all-to-all-start = ((bf16[32,2,4,32,1,128]{5,1,3,2,4,0:T(2,128)(2,1)}), bf16[32,2,4,32,1,128]{5,1,3,2,4,0:T(2,128)(2,1)S(1)}, u32[]{:S(2)}, u32[]{:S(2)}) async-start(bf16[32,2,4,32,1,128]{5,1,3,2,4,0:T(2,128)(2,1)} %copy.28), calls=%async_computation | async-start | bytes 4194304 | tf_op jit(solution)/shard_map/all_to_all | solution.py:28
  164.3 11.1 %collective-permute-start.2 = (f32[4,32,1]{1,0,2:T(4,128)S(1)}, f32[4,32,1]{1,0,2:T(4,128)S(1)}, u32[]{:S(2)}, u32[]{:S(2)}) collective-permute-start(f32[4,32,1]{1,0,2:T(4,128)S(1)} %get-tuple-element.139), channel_id=1, source_target_pairs={{0,4},{4,8},{8,12},{12,16},{16,20},{20,24},{24,28},{28,32},{32,36}... | collective-permute-start | bytes 1544 | tf_op jit(solution)/shard_map/ppermute | solution.py:41
  164.5 13.9 %collective-permute-start = (f32[4,32,1]{1,0,2:T(4,128)S(1)}, f32[4,32,1]{1,0,2:T(4,128)S(1)}, u32[]{:S(2)}, u32[]{:S(2)}) collective-permute-start(f32[4,32,1]{1,0,2:T(4,128)S(1)} %get-tuple-element.139), channel_id=1, source_target_pairs={{0,252},{4,0},{8,4},{12,8},{16,12},{20,16},{24,20},{28,24},{32,28}... | collective-permute-start | bytes 1544 | tf_op jit(solution)/shard_map/ppermute | solution.py:41
  175.5 7.7 %collective-permute-start.3 = (f32[4,32,1]{1,0,2:T(4,128)S(1)}, f32[4,32,1]{1,0,2:T(4,128)S(1)}, u32[]{:S(2)}, u32[]{:S(2)}) collective-permute-start(f32[4,32,1]{1,0,2:T(4,128)S(1)} %collective-permute-done.2), channel_id=1, source_target_pairs={{0,1},{1,2},{2,3},{4,5},{5,6},{6,7},{8,9},{9,10},{10,11},{12,13},{... | collective-permute-start | bytes 1544 | tf_op jit(solution)/shard_map/ppermute | solution.py:47
  178.4 5.5 %collective-permute-start.1 = (f32[4,32,1]{1,0,2:T(4,128)S(1)}, f32[4,32,1]{1,0,2:T(4,128)S(1)}, u32[]{:S(2)}, u32[]{:S(2)}) collective-permute-start(f32[4,32,1]{1,0,2:T(4,128)S(1)} %collective-permute-done), channel_id=1, source_target_pairs={{1,0},{2,1},{3,2},{5,4},{6,5},{7,6},{9,8},{10,9},{11,10},{13,12},{... | collective-permute-start | bytes 1544 | tf_op jit(solution)/shard_map/ppermute | solution.py:47
where the time goes:
time: 185 us; the launch traced here: 184 us
  waiting for transfers between devices  55.8 us (30%)
  local copies, waits for them, and re-layouts  50 us (27%)
  other arithmetic  43.7 us (24%)
  starting transfers between devices  28.7 us (16%)
  blocking collectives  5.42 us (3%)
    all_to_all x1, waiting for transfers between devices, exchange_in_order(): result = lax.all_to_all(result, axes[k], k, k, tiled=True)  53.8 us
    gather x4, local copies, waits for them, and re-layouts, one_level(): window = lax.dynamic_slice_in_dim(block, window_base, WINDOW, 1)  32.6 us
    reduce_sum x4, other arithmetic, one_level(): jnp.sum(jnp.where(steps == offset, window, zero).astype(jnp.float32), axi...  28.4 us
    all_to_all x1, starting transfers between devices, exchange_in_order(): result = lax.all_to_all(result, axes[k], k, k, tiled=True)  13 us
    ppermute x2, starting transfers between devices, shifted(): return lax.ppermute(value, axis, pairs)  9.87 us
    unnamed x1, local copies, waits for them, and re-layouts  9.63 us
    ppermute x2, starting transfers between devices, shifted_2(): return lax.ppermute(block, axis, route)  5.83 us
    all_to_all x1, blocking collectives, exchange_in_order(): result = lax.all_to_all(result, axes[k], k, k, tiled=True)  5.42 us
  transfers between devices with their start and end apart: 5, of which 3 were waited for; matrix products, arithmetic and copies ran while one was open for 1% of the time, Pallas kernels for 0%

commit v1 on v0

v1 whole, which is shorter than its diff:
```python
import functools

import jax
import jax.numpy as jnp
from jax import lax
from jax.experimental import pallas as pl
from jax.experimental.pallas import tpu as pltpu
from jax.sharding import Mesh
from jax.sharding import PartitionSpec as P

WINDOW = 16
LON = ("lon_0", "lon_1", "lon_2", "lon_3")
LAT_LON = ("lat", "lon_0", "lon_1", "lon_2", "lon_3")
AXES = ("lon_0", "lon_1", "lon_2", "lon_3", "lat")
MESH_ID = pl.DeviceIdType.MESH
PEERS = 64
GROUPS = 4
ROWS = 16
LANES = 128


def device_of(lon, lat):
    return (lon // 16, (lon // 8) % 2, (lon // 2) % 4, lon % 2, lat)


def kernel(
    fields, bracket, fraction, out, zonal_out, merid_out,
    fbuf, bbuf, wbuf, tbuf, send, zrow, zprev, znext,
    in_sem, send_sem, recv_sem, zsend_sem, zrecv_sem,
):
    nvar = fields.shape[0]
    levels = fields.shape[1]
    plevs = bracket.shape[0]
    step = levels // plevs
    planes = nvar * plevs
    lon_place = (
        (lax.axis_index("lon_0") * 2 + lax.axis_index("lon_1")) * 4 + lax.axis_index("lon_2")
    ) * 2 + lax.axis_index("lon_3")
    lat_place = lax.axis_index("lat")
    row = lat_place * PEERS + lon_place
    next_row = (row + 1) % (4 * PEERS)
    prev_row = (row + 4 * PEERS - 1) % (4 * PEERS)
    next_device = device_of(next_row % PEERS, next_row // PEERS)
    prev_device = device_of(prev_row % PEERS, prev_row // PEERS)

    def group_of(k):
        return (lon_place // ROWS + k) % GROUPS

    def loads(k):
        rows = pl.ds(pl.multiple_of(group_of(k) * ROWS, ROWS), ROWS)
        return (
            pltpu.make_async_copy(fields.at[:, :, rows, :], fbuf.at[k], in_sem.at[k, 0]),
            pltpu.make_async_copy(bracket.at[:, rows, :], bbuf.at[k], in_sem.at[k, 1]),
            pltpu.make_async_copy(fraction.at[:, rows, :], wbuf.at[k], in_sem.at[k, 2]),
        )

    for k in range(GROUPS):
        for copy in loads(k):
            copy.start()

    barrier = pltpu.get_barrier_semaphore()

    def greet(i, carry):
        lon = (lon_place + i) % PEERS
        pl.semaphore_signal(barrier, inc=1, device_id=device_of(lon, lat_place), device_id_type=MESH_ID)
        return carry

    lax.fori_loop(1, PEERS, greet, 0)
    pl.semaphore_signal(barrier, inc=1, device_id=next_device, device_id_type=MESH_ID)
    pl.semaphore_signal(barrier, inc=1, device_id=prev_device, device_id_type=MESH_ID)

    for k in range(GROUPS):
        for copy in loads(k):
            copy.wait()

        def one_level(p, carry, k=k):
            base = jnp.minimum(p * step, levels - WINDOW)
            offset = (bbuf[k, p] - base).astype(jnp.float32).astype(jnp.bfloat16)
            eight = offset >= 8
            offset = jnp.where(eight, offset - 8, offset)
            four = offset >= 4
            offset = jnp.where(four, offset - 4, offset)
            two = offset >= 2
            offset = jnp.where(two, offset - 2, offset)
            one = offset >= 1
            weight = wbuf[k, p].astype(jnp.float32)
            for v in range(nvar):
                w = [fbuf[k, v, base + j] for j in range(WINDOW)]
                w = [jnp.where(eight, w[j + 8], w[j]) for j in range(8)] + [w[8]]
                w = [jnp.where(four, w[j + 4], w[j]) for j in range(5)]
                w = [jnp.where(two, w[j + 2], w[j]) for j in range(3)]
                lower = jnp.where(one, w[1], w[0]).astype(jnp.float32)
                upper = jnp.where(one, w[2], w[1]).astype(jnp.float32)
                value = lower + weight * (upper - lower)
                at = pl.multiple_of((v * plevs + p) * 8, 8)
                tbuf[0, pl.ds(at, 8), :] = value[:8]
                tbuf[1, pl.ds(at, 8), :] = value[8:]
            return carry

        lax.fori_loop(0, plevs, one_level, 0)

        def one_row(r, carry, k=k):
            for half in range(2):
                for q in range(planes // 16):
                    block = tbuf[half, pl.ds(q * 128 + r, 16, stride=8), :]
                    send[k, half * 8 + r, q * 16 : (q + 1) * 16, :] = block.astype(jnp.bfloat16)
            return carry

        lax.fori_loop(0, 8, one_row, 0)

        if k == 0:
            pl.semaphore_wait(barrier, PEERS + 1)
            mine = send[0, lon_place % ROWS]
            out[:, pl.ds(pl.multiple_of(lon_place * LANES, LANES), LANES)] = mine

        def one_send(r, carry, k=k):
            lon = group_of(k) * ROWS + (r + lon_place) % ROWS

            @pl.when(lon != lon_place)
            def _():
                pltpu.make_async_remote_copy(
                    src_ref=send.at[k, lon % ROWS],
                    dst_ref=out.at[:, pl.ds(pl.multiple_of(lon_place * LANES, LANES), LANES)],
                    send_sem=send_sem,
                    recv_sem=recv_sem,
                    device_id=device_of(lon, lat_place),
                    device_id_type=MESH_ID,
                ).start()

            return carry

        lax.fori_loop(0, ROWS, one_send, 0)

    arrived = out.at[:, pl.ds(0, (PEERS - 1) * LANES)]
    pltpu.make_async_copy(arrived, arrived, recv_sem).wait()

    def add_block(i, total):
        block = out[:, pl.ds(pl.multiple_of(i * LANES, LANES), LANES)]
        return total + block.astype(jnp.float32)

    total = lax.fori_loop(0, PEERS, add_block, jnp.zeros((planes, LANES), jnp.float32))
    mean = jnp.sum(total.T, axis=0, keepdims=True) / jnp.float32(PEERS * LANES)
    zrow[...] = jnp.broadcast_to(mean, zrow.shape)

    to_next = pltpu.make_async_remote_copy(
        src_ref=zrow, dst_ref=zprev, send_sem=zsend_sem.at[0], recv_sem=zrecv_sem.at[0],
        device_id=next_device, device_id_type=MESH_ID,
    )
    to_prev = pltpu.make_async_remote_copy(
        src_ref=zrow, dst_ref=znext, send_sem=zsend_sem.at[1], recv_sem=zrecv_sem.at[1],
        device_id=prev_device, device_id_type=MESH_ID,
    )
    to_next.start()
    to_prev.start()
    for v in range(nvar):
        zonal_out[v] = mean[:, v * plevs : (v + 1) * plevs]
    sent = send.at[:, :, pl.ds(0, planes), :]
    all_sent = out.at[:, pl.ds(0, (PEERS - 1) * LANES)]
    pltpu.make_async_copy(all_sent, all_sent, send_sem).wait()
    to_next.wait()
    to_prev.wait()
    above = znext[0:1, :]
    below = zprev[0:1, :]
    slope = jnp.where(
        row == 0,
        above - mean,
        jnp.where(row == 4 * PEERS - 1, mean - below, 0.5 * (above - below)),
    )
    for v in range(nvar):
        merid_out[v] = slope[:, v * plevs : (v + 1) * plevs]


def shards(fields, bracket, fraction):
    nvar, levels, rows, lanes = fields.shape
    plevs = bracket.shape[0]
    planes = nvar * plevs
    hbm = pl.BlockSpec(memory_space=pltpu.MemorySpace.HBM)
    vmem = pl.BlockSpec(memory_space=pltpu.VMEM)
    on_pressure, zonal, merid = pl.pallas_call(
        kernel,
        name="relay",
        out_shape=(
            jax.ShapeDtypeStruct((planes, PEERS * LANES), jnp.bfloat16),
            jax.ShapeDtypeStruct((nvar, 1, plevs), jnp.float32),
            jax.ShapeDtypeStruct((nvar, 1, plevs), jnp.float32),
        ),
        in_specs=[hbm] * 3,
        out_specs=(vmem, vmem, vmem),
        scratch_shapes=[
            pltpu.VMEM((GROUPS, nvar, levels, ROWS, lanes), jnp.bfloat16),
            pltpu.VMEM((GROUPS, plevs, ROWS, lanes), jnp.int32),
            pltpu.VMEM((GROUPS, plevs, ROWS, lanes), jnp.bfloat16),
            pltpu.VMEM((2, planes * 8, lanes), jnp.float32),
            pltpu.VMEM((GROUPS, ROWS, planes, lanes), jnp.bfloat16),
            pltpu.VMEM((8, planes), jnp.float32),
            pltpu.VMEM((8, planes), jnp.float32),
            pltpu.VMEM((8, planes), jnp.float32),
            pltpu.SemaphoreType.DMA((GROUPS, 3)),
            pltpu.SemaphoreType.DMA,
            pltpu.SemaphoreType.DMA,
            pltpu.SemaphoreType.DMA((2,)),
            pltpu.SemaphoreType.DMA((2,)),
        ],
        compiler_params=pltpu.CompilerParams(
            collective_id=0, has_side_effects=True, vmem_limit_bytes=(64 * 1024 - 64 - 2048 - 64) * 1024
        ),
    )(fields, bracket, fraction)
    return (
        on_pressure.reshape(nvar, plevs, 1, PEERS * LANES),
        zonal.transpose(0, 2, 1),
        merid.transpose(0, 2, 1),
    )


def solution(mesh):
    finer = Mesh(
        mesh.devices.reshape(4, 2, 4, 2, mesh.shape["lat"]),
        AXES,
    )
    in_specs = (P(None, None, "lat", LON), P(None, "lat", LON), P(None, "lat", LON))
    out_specs = (P(None, None, LAT_LON, None), P(None, None, LAT_LON), P(None, None, LAT_LON))
    return jax.shard_map(
        shards, mesh=finer, in_specs=in_specs, out_specs=out_specs, check_vma=False
    )
```

time: 185 us -> 78.5 us (0.42)
  Pallas kernels: 0 us -> 72.5 us
  waiting for transfers between devices: 55.8 us -> 0 us
  local copies, waits for them, and re-layouts: 50 us -> 4.26 us
  other arithmetic: 43.7 us -> 0 us
  starting transfers between devices: 28.7 us -> 0 us
  blocking collectives: 5.42 us -> 0 us
    pallas_call x0 -> x1, Pallas kernels: none -> 72.5 us  [shards(): pl.pallas_call(kernel, name='relay', out_shape=(jax.ShapeDtypeStruct((pla...]
    all_to_all x1 -> x0, waiting for transfers between devices: 53.8 us -> none  [exchange_in_order(): result = lax.all_to_all(result, axes[k], k, k, tiled=True)]
    gather x4 -> x0, local copies, waits for them, and re-layouts: 32.6 us -> none  [one_level(): window = lax.dynamic_slice_in_dim(block, window_base, WINDOW, 1)]
    reduce_sum x5 -> x0, other arithmetic: 28.8 us -> none  [the longest x4 28.4 us: one_level(): jnp.sum(jnp.where(steps == offset, window, zero).astype(jnp.float32), axi...]
    ppermute x4 -> x0, starting transfers between devices: 15.7 us -> none  [the longest x2 9.87 us: shifted(): return lax.ppermute(value, axis, pairs)]
    all_to_all x1 -> x0, starting transfers between devices: 13 us -> none  [exchange_in_order(): result = lax.all_to_all(result, axes[k], k, k, tiled=True)]
    reshape x2 -> x0, local copies, waits for them, and re-layouts: 5.56 us -> none  [the longest x1 3.69 us: exchange_in_order(): result = blocks.reshape(*(lax.axis_size(a) for a in axes), *inside)]
    all_to_all x1 -> x0, blocking collectives: 5.42 us -> none  [exchange_in_order(): result = lax.all_to_all(result, axes[k], k, k, tiled=True)]
  transfers between devices with their start and end apart: 5 -> 0, of which waited for: 3 -> 0; matrix products, arithmetic and copies ran while one was open for 1% -> 0% of each run, Pallas kernels for 0% -> 0%
where the time goes in v1:
time: 78.5 us; the launch traced here: 77.4 us
  Pallas kernels  72.5 us (92%)
  local copies, waits for them, and re-layouts  4.26 us (5%)
    pallas_call x1, Pallas kernels, shards(): pl.pallas_call(kernel, name='relay', out_shape=(jax.ShapeDtypeStruct((pla...  72.5 us
    unnamed x7, local copies, waits for them, and re-layouts  4.26 us

profile of v1, /device:TPU:32, one launch (start us, length us, event | category | flops | bytes accessed | tf_op | source)
XLA Modules:
  0.0 77.4 jit_solution(1508991503558827871)
XLA Ops:
  0.6 72.5 %relay.1 = (bf16[128,8192]{1,0:T(8,128)(2,1)}, f32[4,1,32]{2,1,0:T(1,128)}, f32[4,1,32]{2,1,0:T(1,128)}) custom-call(bf16[4,128,64,128]{3,2,1,0:T(8,128)(2,1)} %fields.1, s32[32,64,128]{2,1,0:T(8,128)} %bracket.1, bf16[32,64,128]{2,1,0:T(8,128)(2,1)} %fraction.1), custom_call_target="tpu_custom_call" | custom-call | tf_op jit(solution)/shard_map/relay/pallas_call | solution.py:179
  73.1 0.0 copy-start.1
  73.1 0.0 copy-start
  73.1 3.1 %copy.12 = bf16[4,32,1,8192]{3,1,2,0:T(8,128)(2,1)} copy(bf16[4,32,1,8192]{3,1,2,0:T(8,128)(2,1)} %bitcast.9) | data formatting | bytes 4194304
  76.2 0.0 copy-done.1
  76.2 0.6 copy.13
  76.8 0.0 copy-done
  76.8 0.6 copy.14
Async XLA Ops:
  73.1 3.1 %copy-start.1 = (f32[4,1,32]{2,1,0:T(1,128)S(1)}, f32[4,1,32]{2,1,0:T(1,128)}, u32[]{:S(2)}) copy-start(f32[4,1,32]{2,1,0:T(1,128)} %get-tuple-element.7) | copy-start | bytes 1540
  73.1 3.7 %copy-start = (f32[4,1,32]{2,1,0:T(1,128)S(1)}, f32[4,1,32]{2,1,0:T(1,128)}, u32[]{:S(2)}) copy-start(f32[4,1,32]{2,1,0:T(1,128)} %get-tuple-element.8) | copy-start | bytes 1540

commit v2 on v1

--- a/solution.py
+++ b/solution.py
@@ -17,6 +17,8 @@
 GROUPS = 4
 ROWS = 16
 LANES = 128
+ROOM_KIB = 15000
+PIECES = 2
 
 
 def device_of(lon, lat):
@@ -25,8 +27,8 @@
 
 def kernel(
     fields, bracket, fraction, out, zonal_out, merid_out,
-    fbuf, bbuf, wbuf, tbuf, send, zrow, zprev, znext,
-    in_sem, send_sem, recv_sem, zsend_sem, zrecv_sem,
+    fbuf, bbuf, wbuf, tbuf, send, part, gathered, band, sums,
+    in_sem, send_sem, recv_sem, part_send, part_recv, sums_send, sums_recv,
 ):
     nvar = fields.shape[0]
     levels = fields.shape[1]
@@ -38,10 +40,8 @@
     ) * 2 + lax.axis_index("lon_3")
     lat_place = lax.axis_index("lat")
     row = lat_place * PEERS + lon_place
-    next_row = (row + 1) % (4 * PEERS)
-    prev_row = (row + 4 * PEERS - 1) % (4 * PEERS)
-    next_device = device_of(next_row % PEERS, next_row // PEERS)
-    prev_device = device_of(prev_row % PEERS, prev_row // PEERS)
+    mine_m = lon_place // 8
+    mine_j = lon_place % 8
 
     def group_of(k):
         return (lon_place // ROWS + k) % GROUPS
@@ -66,14 +66,32 @@
         return carry
 
     lax.fori_loop(1, PEERS, greet, 0)
-    pl.semaphore_signal(barrier, inc=1, device_id=next_device, device_id_type=MESH_ID)
-    pl.semaphore_signal(barrier, inc=1, device_id=prev_device, device_id_type=MESH_ID)
-
-    for k in range(GROUPS):
+
+    @pl.when(lon_place == 0)
+    def _():
+        def greet_below(m, carry):
+            device = device_of(m * 8 + 7, (lat_place + 3) % 4)
+            pl.semaphore_signal(barrier, inc=1, device_id=device, device_id_type=MESH_ID)
+            return carry
+
+        lax.fori_loop(0, 8, greet_below, 0)
+
+    @pl.when(lon_place == PEERS - 1)
+    def _():
+        def greet_above(m, carry):
+            device = device_of(m * 8, (lat_place + 1) % 4)
+            pl.semaphore_signal(barrier, inc=1, device_id=device, device_id_type=MESH_ID)
+            return carry
+
+        lax.fori_loop(0, 8, greet_above, 0)
+
+    ones = jnp.ones((16, LANES), jnp.bfloat16)
+
+    def compute(k):
         for copy in loads(k):
             copy.wait()
 
-        def one_level(p, carry, k=k):
+        def one_level(p, carry):
             base = jnp.minimum(p * step, levels - WINDOW)
             offset = (bbuf[k, p] - base).astype(jnp.float32).astype(jnp.bfloat16)
             eight = offset >= 8
@@ -99,22 +117,24 @@
 
         lax.fori_loop(0, plevs, one_level, 0)
 
-        def one_row(r, carry, k=k):
+        def one_row(r, carry):
             for half in range(2):
                 for q in range(planes // 16):
                     block = tbuf[half, pl.ds(q * 128 + r, 16, stride=8), :]
                     send[k, half * 8 + r, q * 16 : (q + 1) * 16, :] = block.astype(jnp.bfloat16)
+            for half in range(2):
+                total = lax.dot_general(
+                    ones, send[k, half * 8 + r], (((1,), (1,)), ((), ())),
+                    preferred_element_type=jnp.float32,
+                )
+                part[r, group_of(k) * 2 + half] = total[0:1]
             return carry
 
         lax.fori_loop(0, 8, one_row, 0)
 
-        if k == 0:
-            pl.semaphore_wait(barrier, PEERS + 1)
-            mine = send[0, lon_place % ROWS]
-            out[:, pl.ds(pl.multiple_of(lon_place * LANES, LANES), LANES)] = mine
-
-        def one_send(r, carry, k=k):
-            lon = group_of(k) * ROWS + (r + lon_place) % ROWS
+    def send_group(k):
+        def one_send(r, carry):
+            lon = group_of(k) * ROWS + (r + (mine_m + 1) % 2 * 8) % ROWS
 
             @pl.when(lon != lon_place)
             def _():
@@ -131,43 +151,97 @@
 
         lax.fori_loop(0, ROWS, one_send, 0)
 
-    arrived = out.at[:, pl.ds(0, (PEERS - 1) * LANES)]
-    pltpu.make_async_copy(arrived, arrived, recv_sem).wait()
-
-    def add_block(i, total):
-        block = out[:, pl.ds(pl.multiple_of(i * LANES, LANES), LANES)]
-        return total + block.astype(jnp.float32)
-
-    total = lax.fori_loop(0, PEERS, add_block, jnp.zeros((planes, LANES), jnp.float32))
-    mean = jnp.sum(total.T, axis=0, keepdims=True) / jnp.float32(PEERS * LANES)
-    zrow[...] = jnp.broadcast_to(mean, zrow.shape)
-
-    to_next = pltpu.make_async_remote_copy(
-        src_ref=zrow, dst_ref=zprev, send_sem=zsend_sem.at[0], recv_sem=zrecv_sem.at[0],
-        device_id=next_device, device_id_type=MESH_ID,
-    )
-    to_prev = pltpu.make_async_remote_copy(
-        src_ref=zrow, dst_ref=znext, send_sem=zsend_sem.at[1], recv_sem=zrecv_sem.at[1],
-        device_id=prev_device, device_id_type=MESH_ID,
-    )
-    to_next.start()
-    to_prev.start()
-    for v in range(nvar):
-        zonal_out[v] = mean[:, v * plevs : (v + 1) * plevs]
-    sent = send.at[:, :, pl.ds(0, planes), :]
-    all_sent = out.at[:, pl.ds(0, (PEERS - 1) * LANES)]
-    pltpu.make_async_copy(all_sent, all_sent, send_sem).wait()
-    to_next.wait()
-    to_prev.wait()
-    above = znext[0:1, :]
-    below = zprev[0:1, :]
+    compute(0)
+    out[:, pl.ds(pl.multiple_of(lon_place * LANES, LANES), LANES)] = send[0, lon_place % ROWS]
+    pl.semaphore_wait(
+        barrier,
+        PEERS - 1 + (mine_j == 0).astype(jnp.int32) + (mine_j == 7).astype(jnp.int32),
+    )
+    send_group(0)
+    for k in range(1, GROUPS):
+        compute(k)
+
+    def send_part(i, carry):
+        j = (mine_j + i) % 8
+        pltpu.make_async_remote_copy(
+            src_ref=part.at[j],
+            dst_ref=gathered.at[mine_j],
+            send_sem=part_send,
+            recv_sem=part_recv,
+            device_id=device_of(mine_m * 8 + j, lat_place),
+            device_id_type=MESH_ID,
+        ).start()
+        return carry
+
+    lax.fori_loop(1, 8, send_part, 0)
+    gathered[mine_j] = part[mine_j]
+    send_group(1)
+    seven = gathered.at[pl.ds(0, 7)]
+    pltpu.make_async_copy(seven, seven, part_recv).wait()
+    subtotal = gathered[0]
+    for j in range(1, 8):
+        subtotal = subtotal + gathered[j]
+    band[...] = subtotal
+
+    def send_sums(m, carry):
+        here = lat_place * PEERS + m * 8 + mine_j
+        for shift in (-1, 0, 1):
+            there = (here + shift + 4 * PEERS) % (4 * PEERS)
+
+            @pl.when(there != row)
+            def _(shift=shift, there=there):
+                pltpu.make_async_remote_copy(
+                    src_ref=band.at[m],
+                    dst_ref=sums.at[(1 - shift) * 8 + mine_m],
+                    send_sem=sums_send,
+                    recv_sem=sums_recv,
+                    device_id=device_of(there % PEERS, there // PEERS),
+                    device_id_type=MESH_ID,
+                ).start()
+
+        return carry
+
+    lax.fori_loop(0, 8, send_sums, 0)
+    sums[8 + mine_m] = band[mine_m]
+    for k in range(2, GROUPS):
+        send_group(k)
+
+    most = sums.at[pl.ds(0, 23)]
+    pltpu.make_async_copy(most, most, sums_recv).wait()
+    means = []
+    for slot in range(3):
+        total = sums[slot * 8]
+        for m in range(1, 8):
+            total = total + sums[slot * 8 + m]
+        means.append(total / jnp.float32(PEERS * LANES))
+    below, mean, above = means
     slope = jnp.where(
         row == 0,
         above - mean,
         jnp.where(row == 4 * PEERS - 1, mean - below, 0.5 * (above - below)),
     )
     for v in range(nvar):
+        zonal_out[v] = mean[:, v * plevs : (v + 1) * plevs]
         merid_out[v] = slope[:, v * plevs : (v + 1) * plevs]
+    pltpu.make_async_copy(seven, seven, part_send).wait()
+    pltpu.make_async_copy(most, most, sums_send).wait()
+    arrived = out.at[:, pl.ds(0, (PEERS - 1) * LANES)]
+    pltpu.make_async_copy(arrived, arrived, send_sem).wait()
+    pltpu.make_async_copy(arrived, arrived, recv_sem).wait()
+
+
+def finish(relaid, zonal, merid, out, zonal_out, merid_out, sem):
+    copies = [
+        pltpu.make_async_copy(zonal, zonal_out, sem.at[0]),
+        pltpu.make_async_copy(merid, merid_out, sem.at[1]),
+    ]
+    for i in range(PIECES):
+        rows = pl.ds(i * relaid.shape[0] // PIECES, relaid.shape[0] // PIECES)
+        copies.append(pltpu.make_async_copy(relaid.at[rows], out.at[rows], sem.at[i + 2]))
+    for copy in copies:
+        copy.start()
+    for copy in copies:
+        copy.wait()
 
 
 def shards(fields, bracket, fraction):
@@ -176,6 +250,10 @@
     planes = nvar * plevs
     hbm = pl.BlockSpec(memory_space=pltpu.MemorySpace.HBM)
     vmem = pl.BlockSpec(memory_space=pltpu.VMEM)
+    args = [
+        pltpu.with_memory_space_constraint(x, pltpu.MemorySpace.HBM)
+        for x in (fields, bracket, fraction)
+    ]
     on_pressure, zonal, merid = pl.pallas_call(
         kernel,
         name="relay",
@@ -192,19 +270,35 @@
             pltpu.VMEM((GROUPS, plevs, ROWS, lanes), jnp.bfloat16),
             pltpu.VMEM((2, planes * 8, lanes), jnp.float32),
             pltpu.VMEM((GROUPS, ROWS, planes, lanes), jnp.bfloat16),
-            pltpu.VMEM((8, planes), jnp.float32),
-            pltpu.VMEM((8, planes), jnp.float32),
-            pltpu.VMEM((8, planes), jnp.float32),
+            pltpu.VMEM((8, 8, 1, planes), jnp.float32),
+            pltpu.VMEM((8, 8, 1, planes), jnp.float32),
+            pltpu.VMEM((8, 1, planes), jnp.float32),
+            pltpu.VMEM((24, 1, planes), jnp.float32),
             pltpu.SemaphoreType.DMA((GROUPS, 3)),
             pltpu.SemaphoreType.DMA,
             pltpu.SemaphoreType.DMA,
-            pltpu.SemaphoreType.DMA((2,)),
-            pltpu.SemaphoreType.DMA((2,)),
+            pltpu.SemaphoreType.DMA,
+            pltpu.SemaphoreType.DMA,
+            pltpu.SemaphoreType.DMA,
+            pltpu.SemaphoreType.DMA,
         ],
         compiler_params=pltpu.CompilerParams(
-            collective_id=0, has_side_effects=True, vmem_limit_bytes=(64 * 1024 - 64 - 2048 - 64) * 1024
+            collective_id=0, has_side_effects=True, vmem_limit_bytes=(64 * 1024 - ROOM_KIB) * 1024
         ),
-    )(fields, bracket, fraction)
+    )(*args)
+    on_pressure, zonal, merid = pl.pallas_call(
+        finish,
+        name="finish",
+        out_shape=(
+            jax.ShapeDtypeStruct((planes, PEERS * LANES), jnp.bfloat16),
+            jax.ShapeDtypeStruct((nvar, 1, plevs), jnp.float32),
+            jax.ShapeDtypeStruct((nvar, 1, plevs), jnp.float32),
+        ),
+        in_specs=[pl.BlockSpec(memory_space=pl.ANY)] * 3,
+        out_specs=(hbm, hbm, hbm),
+        scratch_shapes=[pltpu.SemaphoreType.DMA((PIECES + 2,))],
+        compiler_params=pltpu.CompilerParams(vmem_limit_bytes=1 * 2**20),
+    )(on_pressure, zonal, merid)
     return (
         on_pressure.reshape(nvar, plevs, 1, PEERS * LANES),
         zonal.transpose(0, 2, 1),

time: 78.5 us -> 65.4 us (0.83)
  the two profiles are of different devices: /device:TPU:32 before, /device:TPU:121 now
where the time goes in v2:
time: 65.4 us; the launch traced here: 65.3 us
  Pallas kernels  64.7 us (99%)
    pallas_call x1, Pallas kernels, shards(): pl.pallas_call(kernel, name='relay', out_shape=(jax.ShapeDtypeStruct((pla...  63.3 us
    pallas_call x1, Pallas kernels, shards(): pl.pallas_call(finish, name='finish', out_shape=(jax.ShapeDtypeStruct((pl...  1.36 us

profile of v2, /device:TPU:121, one launch (start us, length us, event | category | flops | bytes accessed | tf_op | source)
XLA Modules:
  0.0 65.3 jit_solution(6116502932870274887)
XLA Ops:
  0.6 63.3 %relay.1 = (bf16[128,8192]{1,0:T(8,128)(2,1)S(1)}, f32[4,1,32]{2,1,0:T(1,128)S(1)}, f32[4,1,32]{2,1,0:T(1,128)S(1)}) custom-call(bf16[4,128,64,128]{3,2,1,0:T(8,128)(2,1)} %fields.1, s32[32,64,128]{2,1,0:T(8,128)} %bracket.1, bf16[32,64,128]{2,1,0:T(8,128)(2,1)} %fraction.1), custom_call_target="tpu_custom_call" | custom-call | tf_op jit(solution)/shard_map/relay/pallas_call | solution.py:257
  64.0 1.4 %finish.1 = (bf16[128,8192]{1,0:T(8,128)(2,1)}, f32[4,1,32]{2,1,0:T(1,128)}, f32[4,1,32]{2,1,0:T(1,128)}) custom-call(bf16[128,8192]{1,0:T(8,128)(2,1)S(1)} %get-tuple-element.9.relaid, f32[4,1,32]{2,1,0:T(1,128)S(1)} %get-tuple-element.10.zonal, f32[4,1,32]{2,1,0:T(1,128)S(1)} %get-tuple-element.11.merid), custom_call_target="tpu_custom_call" | custom-call | tf_op jit(solution)/shard_map/finish/pallas_call | solution.py:289

commit v3 on v2

--- a/solution.py
+++ b/solution.py
@@ -19,6 +19,7 @@
 LANES = 128
 ROOM_KIB = 15000
 PIECES = 2
+X_ORDER = (1, 3, 2, 0)
 
 
 def device_of(lon, lat):
@@ -44,7 +45,7 @@
     mine_j = lon_place % 8
 
     def group_of(k):
-        return (lon_place // ROWS + k) % GROUPS
+        return (lon_place // ROWS + X_ORDER[k]) % GROUPS
 
     def loads(k):
         rows = pl.ds(pl.multiple_of(group_of(k) * ROWS, ROWS), ROWS)
@@ -132,9 +133,16 @@
 
         lax.fori_loop(0, 8, one_row, 0)
 
-    def send_group(k):
-        def one_send(r, carry):
-            lon = group_of(k) * ROWS + (r + (mine_m + 1) % 2 * 8) % ROWS
+    place_y = (lon_place // 2) % 4
+    place_c = lon_place % 2
+    place_zh = mine_m % 2
+
+    def send_half(k, cross):
+        def one_send(i, carry):
+            y = (place_y + 1 + i // 2) % 4
+            c = (place_c + i) % 2
+            half = (place_zh + cross) % 2
+            lon = group_of(k) * ROWS + half * 8 + y * 2 + c
 
             @pl.when(lon != lon_place)
             def _():
@@ -149,17 +157,22 @@
 
             return carry
 
-        lax.fori_loop(0, ROWS, one_send, 0)
+        lax.fori_loop(0, 8, one_send, 0)
+
+    def send_group(k):
+        send_half(k, 1)
+        send_half(k, 0)
 
     compute(0)
-    out[:, pl.ds(pl.multiple_of(lon_place * LANES, LANES), LANES)] = send[0, lon_place % ROWS]
     pl.semaphore_wait(
         barrier,
         PEERS - 1 + (mine_j == 0).astype(jnp.int32) + (mine_j == 7).astype(jnp.int32),
     )
-    send_group(0)
+    send_half(0, 1)
     for k in range(1, GROUPS):
         compute(k)
+    mine = send[X_ORDER.index(0), lon_place % ROWS]
+    out[:, pl.ds(pl.multiple_of(lon_place * LANES, LANES), LANES)] = mine
 
     def send_part(i, carry):
         j = (mine_j + i) % 8
@@ -175,7 +188,7 @@
 
     lax.fori_loop(1, 8, send_part, 0)
     gathered[mine_j] = part[mine_j]
-    send_group(1)
+    send_half(1, 1)
     seven = gathered.at[pl.ds(0, 7)]
     pltpu.make_async_copy(seven, seven, part_recv).wait()
     subtotal = gathered[0]
@@ -204,7 +217,9 @@
     lax.fori_loop(0, 8, send_sums, 0)
     sums[8 + mine_m] = band[mine_m]
     for k in range(2, GROUPS):
-        send_group(k)
+        send_half(k, 1)
+    for k in range(GROUPS):
+        send_half(k, 0)
 
     most = sums.at[pl.ds(0, 23)]
     pltpu.make_async_copy(most, most, sums_recv).wait()

time: 65.4 us -> 61.7 us (0.943)
  the two profiles are of different devices: /device:TPU:121 before, /device:TPU:97 now
where the time goes in v3:
time: 61.7 us; the launch traced here: 61.6 us
  Pallas kernels  61 us (99%)
  between operations  0.64 us (1%)
    pallas_call x1, Pallas kernels, shards(): pl.pallas_call(kernel, name='relay', out_shape=(jax.ShapeDtypeStruct((pla...  59.6 us
    pallas_call x1, Pallas kernels, shards(): pl.pallas_call(finish, name='finish', out_shape=(jax.ShapeDtypeStruct((pl...  1.36 us

profile of v3, /device:TPU:97, one launch (start us, length us, event | category | flops | bytes accessed | tf_op | source)
XLA Modules:
  0.0 61.6 jit_solution(14708751168060601826)
XLA Ops:
  0.6 59.6 %relay.1 = (bf16[128,8192]{1,0:T(8,128)(2,1)S(1)}, f32[4,1,32]{2,1,0:T(1,128)S(1)}, f32[4,1,32]{2,1,0:T(1,128)S(1)}) custom-call(bf16[4,128,64,128]{3,2,1,0:T(8,128)(2,1)} %fields.1, s32[32,64,128]{2,1,0:T(8,128)} %bracket.1, bf16[32,64,128]{2,1,0:T(8,128)(2,1)} %fraction.1), custom_call_target="tpu_custom_call" | custom-call | tf_op jit(solution)/shard_map/relay/pallas_call | solution.py:272
  60.3 1.4 %finish.1 = (bf16[128,8192]{1,0:T(8,128)(2,1)}, f32[4,1,32]{2,1,0:T(1,128)}, f32[4,1,32]{2,1,0:T(1,128)}) custom-call(bf16[128,8192]{1,0:T(8,128)(2,1)S(1)} %get-tuple-element.9.relaid, f32[4,1,32]{2,1,0:T(1,128)S(1)} %get-tuple-element.10.zonal, f32[4,1,32]{2,1,0:T(1,128)S(1)} %get-tuple-element.11.merid), custom_call_target="tpu_custom_call" | custom-call | tf_op jit(solution)/shard_map/finish/pallas_call | solution.py:304

commit v4 on v3

--- a/solution.py
+++ b/solution.py
@@ -45,7 +45,7 @@
     mine_j = lon_place % 8
 
     def group_of(k):
-        return (lon_place // ROWS + X_ORDER[k]) % GROUPS
+        return (lon_place // ROWS + GROUPS + (1 - 2 * (lon_place % 2)) * X_ORDER[k]) % GROUPS
 
     def loads(k):
         rows = pl.ds(pl.multiple_of(group_of(k) * ROWS, ROWS), ROWS)
@@ -55,9 +55,8 @@
             pltpu.make_async_copy(fraction.at[:, rows, :], wbuf.at[k], in_sem.at[k, 2]),
         )
 
-    for k in range(GROUPS):
-        for copy in loads(k):
-            copy.start()
+    for copy in loads(0):
+        copy.start()
 
     barrier = pltpu.get_barrier_semaphore()
 
@@ -91,6 +90,9 @@
     def compute(k):
         for copy in loads(k):
             copy.wait()
+        if k + 1 < GROUPS:
+            for copy in loads(k + 1):
+                copy.start()
 
         def one_level(p, carry):
             base = jnp.minimum(p * step, levels - WINDOW)
@@ -149,7 +151,7 @@
                 pltpu.make_async_remote_copy(
                     src_ref=send.at[k, lon % ROWS],
                     dst_ref=out.at[:, pl.ds(pl.multiple_of(lon_place * LANES, LANES), LANES)],
-                    send_sem=send_sem,
+                    send_sem=send_sem.at[k, cross],
                     recv_sem=recv_sem,
                     device_id=device_of(lon, lat_place),
                     device_id_type=MESH_ID,
@@ -159,20 +161,10 @@
 
         lax.fori_loop(0, 8, one_send, 0)
 
-    def send_group(k):
-        send_half(k, 1)
-        send_half(k, 0)
-
-    compute(0)
-    pl.semaphore_wait(
-        barrier,
-        PEERS - 1 + (mine_j == 0).astype(jnp.int32) + (mine_j == 7).astype(jnp.int32),
-    )
-    send_half(0, 1)
-    for k in range(1, GROUPS):
-        compute(k)
-    mine = send[X_ORDER.index(0), lon_place % ROWS]
-    out[:, pl.ds(pl.multiple_of(lon_place * LANES, LANES), LANES)] = mine
+    def wait_sent(k, cross):
+        count = 7 if X_ORDER[k] == 0 and cross == 0 else 8
+        blocks = send.at[k, pl.ds(0, count)]
+        pltpu.make_async_copy(blocks, blocks, send_sem.at[k, cross]).wait()
 
     def send_part(i, carry):
         j = (mine_j + i) % 8
@@ -186,6 +178,17 @@
         ).start()
         return carry
 
+    compute(0)
+    pl.semaphore_wait(
+        barrier,
+        PEERS - 1 + (mine_j == 0).astype(jnp.int32) + (mine_j == 7).astype(jnp.int32),
+    )
+    send_half(0, 1)
+    compute(1)
+    compute(2)
+    compute(3)
+    mine = send[X_ORDER.index(0), lon_place % ROWS]
+    out[:, pl.ds(pl.multiple_of(lon_place * LANES, LANES), LANES)] = mine
     lax.fori_loop(1, 8, send_part, 0)
     gathered[mine_j] = part[mine_j]
     send_half(1, 1)
@@ -216,11 +219,10 @@
 
     lax.fori_loop(0, 8, send_sums, 0)
     sums[8 + mine_m] = band[mine_m]
-    for k in range(2, GROUPS):
-        send_half(k, 1)
+    send_half(2, 1)
+    send_half(3, 1)
     for k in range(GROUPS):
         send_half(k, 0)
-
     most = sums.at[pl.ds(0, 23)]
     pltpu.make_async_copy(most, most, sums_recv).wait()
     means = []
@@ -240,8 +242,10 @@
         merid_out[v] = slope[:, v * plevs : (v + 1) * plevs]
     pltpu.make_async_copy(seven, seven, part_send).wait()
     pltpu.make_async_copy(most, most, sums_send).wait()
+    for k in range(GROUPS):
+        wait_sent(k, 1)
+        wait_sent(k, 0)
     arrived = out.at[:, pl.ds(0, (PEERS - 1) * LANES)]
-    pltpu.make_async_copy(arrived, arrived, send_sem).wait()
     pltpu.make_async_copy(arrived, arrived, recv_sem).wait()
 
 
@@ -290,7 +294,7 @@
             pltpu.VMEM((8, 1, planes), jnp.float32),
             pltpu.VMEM((24, 1, planes), jnp.float32),
             pltpu.SemaphoreType.DMA((GROUPS, 3)),
-            pltpu.SemaphoreType.DMA,
+            pltpu.SemaphoreType.DMA((GROUPS, 2)),
             pltpu.SemaphoreType.DMA,
             pltpu.SemaphoreType.DMA,
             pltpu.SemaphoreType.DMA,

time: 61.7 us -> 61 us (0.989)
  the two profiles are of different devices: /device:TPU:97 before, /device:TPU:65 now
where the time goes in v4:
time: 61 us; the launch traced here: 60.9 us
  Pallas kernels  60.3 us (99%)
  between operations  0.64 us (1%)
    pallas_call x1, Pallas kernels, shards(): pl.pallas_call(kernel, name='relay', out_shape=(jax.ShapeDtypeStruct((pla...  58.9 us
    pallas_call x1, Pallas kernels, shards(): pl.pallas_call(finish, name='finish', out_shape=(jax.ShapeDtypeStruct((pl...  1.36 us

profile of v4, /device:TPU:65, one launch (start us, length us, event | category | flops | bytes accessed | tf_op | source)
XLA Modules:
  0.0 60.9 jit_solution(624191457812562474)
XLA Ops:
  0.6 58.9 %relay.1 = (bf16[128,8192]{1,0:T(8,128)(2,1)S(1)}, f32[4,1,32]{2,1,0:T(1,128)S(1)}, f32[4,1,32]{2,1,0:T(1,128)S(1)}) custom-call(bf16[4,128,64,128]{3,2,1,0:T(8,128)(2,1)} %fields.1, s32[32,64,128]{2,1,0:T(8,128)} %bracket.1, bf16[32,64,128]{2,1,0:T(8,128)(2,1)} %fraction.1), custom_call_target="tpu_custom_call" | custom-call | tf_op jit(solution)/shard_map/relay/pallas_call | solution.py:276
  59.6 1.4 %finish.1 = (bf16[128,8192]{1,0:T(8,128)(2,1)}, f32[4,1,32]{2,1,0:T(1,128)}, f32[4,1,32]{2,1,0:T(1,128)}) custom-call(bf16[128,8192]{1,0:T(8,128)(2,1)S(1)} %get-tuple-element.9.relaid, f32[4,1,32]{2,1,0:T(1,128)S(1)} %get-tuple-element.10.zonal, f32[4,1,32]{2,1,0:T(1,128)S(1)} %get-tuple-element.11.merid), custom_call_target="tpu_custom_call" | custom-call | tf_op jit(solution)/shard_map/finish/pallas_call | solution.py:308
